TPU v7x, 32 devices: a whole 2x2x4 slice. The times are simulated.
32 devices in a mesh: gx: 4 (over z), gy: 4 (over y, x), gz: 2 (over core).
Axes of the slice: x: 2, y: 2, z: 4, core: 2. Of those that a mesh axis runs over, the one named last changes fastest.
Arguments:
- panels: float32 [4, 32768], P(None, ('gy', 'gz')), may hold values from -2 to 3, as said below
- diagonal: float32 [32768], P(('gy', 'gz')), may hold values from 0.5 to 2
- right_side: float32 [32, 32768], P(None, ('gy', 'gz')), may hold values from -6 to 6
- start_guess: float32 [32, 32768], P(None, ('gy', 'gz')), may hold values from -6 to 6
Outputs:
- solution: float32 [32, 32768], P(None, ('gy', 'gz'))
- residual: float32 [32, 32768], P(None, ('gy', 'gz'))
- history: float32 [4, 32], replicated
Inputs may be any that keep to these rules, and one draw needn't show every extreme that they name: `panels`: rows 0 to 2 are centroids of a closed surface around the anchor, row 3 positive areas between 0.3 and 3.
All inputs are finite; a program needn't handle non-finite values.
Results may differ from a plain program's by a relative error of at most 0.00035.
Values sent between devices are 32-bit elements; how exact they have to be, the bound alone decides.
A program may use at most 64 MiB of HBM per device.

v0:
```python
import functools

import jax
import jax.numpy as jnp
from jax import lax
from jax.experimental import pallas as pl
from jax.experimental.pallas import tpu as pltpu
from jax.sharding import PartitionSpec as P

ITERS = 4
soft_sq = 0.0025
PLANE = ("gy", "gz")


def three(value):
    high = lax.reduce_precision(value, 8, 7)
    rest = value - high
    mid = lax.reduce_precision(rest, 8, 7)
    return high, mid, lax.reduce_precision(rest - mid, 8, 7)


def features(row_pan, col_pan):
    left, right = [], []
    for axis in range(3):
        r = three(row_pan[axis])
        c = three(-2.0 * col_pan[axis])
        for i in range(3):
            for j in range(3):
                if i + j < 4:
                    left.append(r[i])
                    right.append(c[j])
    r_sq = three(jnp.sum(row_pan[:3] ** 2, 0))
    c_sq = three(jnp.sum(col_pan[:3] ** 2, 0) + soft_sq)
    one_r, one_c = jnp.ones_like(row_pan[0]), jnp.ones_like(col_pan[0])
    for i in range(3):
        left += [r_sq[i], one_r]
        right += [one_c, c_sq[i]]
    left += [jnp.zeros_like(one_r)] * 2
    right += [jnp.zeros_like(one_c)] * 2
    return jnp.stack(left).astype(jnp.bfloat16), jnp.stack(right).astype(jnp.bfloat16)


def product_kernel(tile, x_ref, left_ref, right_ref, out_ref, parts):
    pieces, cases, width = x_ref.shape

    @pl.when(pl.program_id(0) == 0)
    def _():
        for piece in range(pieces):
            value = x_ref[piece]
            high = value.astype(jnp.bfloat16)
            parts[piece, :cases] = high
            parts[piece, cases:] = (value - high.astype(jnp.float32)).astype(jnp.bfloat16)

    right = right_ref[...]
    cols = right.shape[1]

    def step(piece, carry):
        full, low_sum = carry
        base = pl.multiple_of(piece * width, width)
        for sub in range(width // tile):
            left = left_ref[pl.ds(base + sub * tile, tile), :]
            dist = jnp.dot(left, right, preferred_element_type=jnp.float32)
            value = lax.rsqrt(dist)
            high = value.astype(jnp.bfloat16)
            low = (value - high.astype(jnp.float32)).astype(jnp.bfloat16)
            x_both = parts[piece, :, sub * tile:(sub + 1) * tile]
            full = full + jnp.dot(x_both, high, preferred_element_type=jnp.float32)
            low_sum = low_sum + jnp.dot(x_both[:cases], low, preferred_element_type=jnp.float32)
        return full, low_sum

    full, low_sum = lax.fori_loop(
        0, pieces, step,
        (jnp.zeros((2 * cases, cols), jnp.float32), jnp.zeros((cases, cols), jnp.float32)),
        unroll=True)
    out_ref[0] = full[:cases] + (full[cases:] + low_sum)


def product(x, left, right, parts_out):
    pieces, cases, width = x.shape
    rows, depth = left.shape
    cols = right.shape[1]
    tile = min(256, width)
    wide = cols // parts_out
    step_cols = min(256, wide)
    per = wide // step_cols
    return pl.pallas_call(
        functools.partial(product_kernel, tile),
        grid=(cols // step_cols,),
        out_shape=jax.ShapeDtypeStruct((parts_out, cases, wide), jnp.float32),
        in_specs=[
            pl.BlockSpec((pieces, cases, width), lambda j: (0, 0, 0)),
            pl.BlockSpec((rows, depth), lambda j: (0, 0)),
            pl.BlockSpec((depth, step_cols), lambda j: (0, j)),
        ],
        out_specs=pl.BlockSpec((1, cases, step_cols), lambda j: (j // per, 0, j % per)),
        scratch_shapes=[pltpu.VMEM((pieces, 2 * cases, width), jnp.bfloat16)],
        compiler_params=pltpu.CompilerParams(
            dimension_semantics=("arbitrary",), vmem_limit_bytes=32 * 1024 * 1024),
        cost_estimate=pl.CostEstimate(
            flops=2 * rows * cols * 256, bytes_accessed=4 * rows * cases, transcendentals=rows * cols),
    )(x, left, right)


def on_device(panels, diagonal, right_side, start_guess):
    col_count = panels.shape[1]
    cases = right_side.shape[0]
    depth = lax.axis_size("gx")
    total = col_count * lax.axis_size("gy") * lax.axis_size("gz")
    width = col_count // depth
    mine = lax.axis_index("gx") * width

    def own(value):
        return lax.dynamic_slice_in_dim(value, mine, width, value.ndim - 1)

    pan_own = own(panels)
    diag_own = own(diagonal)[None, :]
    area_own = pan_own[3][None, :]
    scaled_area = area_own * total ** (-0.5)
    row_pan = lax.all_gather(pan_own, PLANE, axis=0)
    row_pan = jnp.swapaxes(row_pan, 0, 1).reshape(4, -1)
    left, right = features(row_pan, panels)
    left = left.T

    def matvec(vector):
        gathered = lax.all_gather(vector * scaled_area, PLANE, axis=0)
        partial_value = product(gathered, left, right, depth)
        summed = lax.psum_scatter(partial_value, "gx", scatter_dimension=0)
        return diag_own * vector + area_own * summed

    solution = own(start_guess)
    residual = own(right_side) - matvec(solution)
    image_res = matvec(residual)
    direction = jnp.zeros_like(residual)
    sdir = jnp.zeros_like(residual)
    zdir = jnp.zeros_like(residual)
    gamma_prev = jnp.ones((cases,), jnp.float32)
    alpha_prev = jnp.ones((cases,), jnp.float32)
    records = []
    for turn_index in range(ITERS):
        sums = jnp.stack([
            jnp.sum(residual * residual, 1),
            jnp.sum(image_res * residual, 1),
            jnp.sum(image_res * image_res, 1),
        ])
        gamma_now, delta_now, omega_now = lax.psum(sums, ("gx", "gy", "gz"))
        last = turn_index == ITERS - 1
        records.append(jnp.sqrt(omega_now / gamma_now))
        if turn_index == 0:
            beta_now = jnp.zeros((cases,), jnp.float32)
            alpha_now = gamma_now / delta_now
        else:
            beta_now = gamma_now / gamma_prev
            alpha_now = gamma_now / (delta_now - beta_now * gamma_now / alpha_prev)
        beta_col = beta_now[:, None]
        alpha_col = alpha_now[:, None]
        sdir_old = sdir
        sdir = image_res + beta_col * sdir_old
        direction = residual + beta_col * direction
        solution = solution + alpha_col * direction
        residual = residual - alpha_col * sdir
        if not last:
            fresh = matvec(image_res)
            zdir = fresh + beta_col * zdir
            image_res = image_res - alpha_col * zdir
        gamma_prev = gamma_now
        alpha_prev = alpha_now
    both = lax.all_gather(jnp.stack([solution, residual]), "gx", axis=2)
    both = both.reshape(2, cases, col_count)
    return (both[0], both[1], jnp.stack(records))


def solution(mesh):
    placed = (P(None, PLANE), P(PLANE), P(None, PLANE), P(None, PLANE))
    return jax.shard_map(
        on_device,
        mesh=mesh,
        in_specs=placed,
        out_specs=(P(None, PLANE), P(None, PLANE), P()),
        check_vma=False,
    )
```

profile of v0, /device:TPU:0, one launch (start us, length us, event | category | flops | bytes accessed | tf_op | source)
XLA Modules:
  0.0 601.1 jit_solution(11034798643353913447)
XLA Ops:
  8.0 1.6 dynamic-slice_multiply_fusion
  11.3 10.7 %all-gather.7 = f32[8,4,1024]{2,1,0:T(4,128)S(1)} all-gather(f32[1,4,1024]{2,1,0:T(4,128)S(1)} %dynamic-slice_bitcast_fusion), channel_id=3, replica_groups=mesh['gx'=4,'gy'=4,'gz'=2] {'gy','gz'}, dimensions={0}, use_global_device_ids=true | all-gather | bytes 147456 | tf_op jit(solution)/shard_map/all_gather | solution.py:119
  22.6 1.5 stack.51
  26.1 10.4 %all-gather.15.cloned.1.call-done = f32[256,1024]{1,0:T(8,128)} async-done(((f32[32,1024]{1,0:T(8,128)}), f32[256,1024]{1,0:T(8,128)}) %all-gather.15.cloned.1.call-update) | async-done | bytes 1048592 | tf_op jit(solution)/shard_map/all_gather | solution.py:125
  36.6 1.2 copy-done
  37.8 43.0 %shard_map.67 = f32[4,32,1024]{2,1,0:T(8,128)} custom-call(f32[8,32,1024]{2,1,0:T(8,128)S(1)} %bitcast.151, bf16[8192,32]{1,0:T(8,128)(2,1)S(1)} %bitcast.146, bf16[32,4096]{1,0:T(8,128)(2,1)S(1)} %stack.53.right_ref), custom_call_target="tpu_custom_call" | custom-call | flops 17179869184 | bytes 1048576 | tf_op jit(solution)/shard_map/pallas_call | solution.py:86
  81.6 21.2 %reduce-scatter.6.cloned.1.call-done = f32[1,32,1024]{2,1,0:T(8,128)} async-done(((f32[4,32,1024]{2,1,0:T(8,128)}), f32[1,32,1024]{2,1,0:T(8,128)}) %reduce-scatter.6.cloned.1.call-update) | async-done | bytes 131088 | tf_op jit(solution)/shard_map/reduce_scatter | solution.py:127
  102.8 1.7 broadcast_multiply_fusion.3
  104.6 22.3 %all-gather.17.cloned.1.call-done = f32[256,1024]{1,0:T(8,128)} async-done(((f32[32,1024]{1,0:T(8,128)}), f32[256,1024]{1,0:T(8,128)}) %all-gather.17.cloned.1.call-update) | async-done | bytes 1048592 | tf_op jit(solution)/shard_map/all_gather | solution.py:125
  127.0 1.2 copy-done.2
  128.2 43.0 %shard_map.68 = f32[4,32,1024]{2,1,0:T(8,128)} custom-call(f32[8,32,1024]{2,1,0:T(8,128)S(1)} %bitcast.153, bf16[8192,32]{1,0:T(8,128)(2,1)S(1)} %bitcast.147, bf16[32,4096]{1,0:T(8,128)(2,1)S(1)} %stack.53.right_ref), custom_call_target="tpu_custom_call" | custom-call | flops 17179869184 | bytes 1048576 | tf_op jit(solution)/shard_map/pallas_call | solution.py:86
  171.3 21.9 %reduce-scatter.8.cloned.1.call-done = f32[1,32,1024]{2,1,0:T(8,128)} async-done(((f32[4,32,1024]{2,1,0:T(8,128)}), f32[1,32,1024]{2,1,0:T(8,128)}) %reduce-scatter.8.cloned.1.call-update) | async-done | bytes 131088 | tf_op jit(solution)/shard_map/reduce_scatter | solution.py:127
  193.2 1.1 multiply_reduce_fusion.11
  195.3 21.9 %all-gather.19.cloned.1.call-done = f32[256,1024]{1,0:T(8,128)} async-done(((f32[32,1024]{1,0:T(8,128)}), f32[256,1024]{1,0:T(8,128)}) %all-gather.19.cloned.1.call-update) | async-done | bytes 1048592 | tf_op jit(solution)/shard_map/all_gather | solution.py:125
  217.1 1.2 copy-done.3
  218.4 43.0 %shard_map.69 = f32[4,32,1024]{2,1,0:T(8,128)} custom-call(f32[8,32,1024]{2,1,0:T(8,128)S(1)} %bitcast.154, bf16[8192,32]{1,0:T(8,128)(2,1)S(1)} %bitcast.148, bf16[32,4096]{1,0:T(8,128)(2,1)S(1)} %stack.53.right_ref), custom_call_target="tpu_custom_call" | custom-call | flops 17179869184 | bytes 1048576 | tf_op jit(solution)/shard_map/pallas_call | solution.py:86
  261.5 39.8 %psum.28 = f32[3,32]{1,0:T(4,128)S(1)} all-reduce(f32[3,32]{1,0:T(4,128)S(1)} %pad_maximum_fusion.1), channel_id=1, replica_groups=mesh['gx'=4,'gy'=4,'gz'=2] {'gx','gy','gz'}, use_global_device_ids=true, to_apply=%region_7.0 | all-reduce | flops 96 | bytes 768 | tf_op jit(solution)/shard_map/psum | solution.py:145
  301.3 1.2 multiply_reduce_fusion.8
  303.2 23.7 %all-gather.21.cloned.1.call-done = f32[256,1024]{1,0:T(8,128)} async-done(((f32[32,1024]{1,0:T(8,128)}), f32[256,1024]{1,0:T(8,128)}) %all-gather.21.cloned.1.call-update) | async-done | bytes 1048592 | tf_op jit(solution)/shard_map/all_gather | solution.py:125
  326.9 1.2 copy-done.4
  328.1 43.0 %shard_map.70 = f32[4,32,1024]{2,1,0:T(8,128)} custom-call(f32[8,32,1024]{2,1,0:T(8,128)S(1)} %bitcast.155, bf16[8192,32]{1,0:T(8,128)(2,1)S(1)} %bitcast.149, bf16[32,4096]{1,0:T(8,128)(2,1)S(1)} %stack.53.right_ref), custom_call_target="tpu_custom_call" | custom-call | flops 17179869184 | bytes 1048576 | tf_op jit(solution)/shard_map/pallas_call | solution.py:86
  371.3 39.8 %psum.29 = f32[3,32]{1,0:T(4,128)S(1)} all-reduce(f32[3,32]{1,0:T(4,128)S(1)} %pad_maximum_fusion.2), channel_id=1, replica_groups=mesh['gx'=4,'gy'=4,'gz'=2] {'gx','gy','gz'}, use_global_device_ids=true, to_apply=%region_12.0 | all-reduce | flops 96 | bytes 768 | tf_op jit(solution)/shard_map/psum | solution.py:145
  411.1 1.2 multiply_reduce_fusion.5
  413.0 23.7 %all-gather.23.cloned.1.call-done = f32[256,1024]{1,0:T(8,128)} async-done(((f32[32,1024]{1,0:T(8,128)}), f32[256,1024]{1,0:T(8,128)}) %all-gather.23.cloned.1.call-update) | async-done | bytes 1048592 | tf_op jit(solution)/shard_map/all_gather | solution.py:125
  436.7 1.2 copy-done.1
  437.9 43.0 %shard_map.71 = f32[4,32,1024]{2,1,0:T(8,128)} custom-call(f32[8,32,1024]{2,1,0:T(8,128)S(1)} %bitcast.152, bf16[8192,32]{1,0:T(8,128)(2,1)S(1)} %bitcast.150, bf16[32,4096]{1,0:T(8,128)(2,1)S(1)} %stack.53.right_ref), custom_call_target="tpu_custom_call" | custom-call | flops 17179869184 | bytes 1048576 | tf_op jit(solution)/shard_map/pallas_call | solution.py:86
  481.0 39.7 %psum.30 = f32[3,32]{1,0:T(4,128)S(1)} all-reduce(f32[3,32]{1,0:T(4,128)S(1)} %pad_maximum_fusion.3), channel_id=1, replica_groups=mesh['gx'=4,'gy'=4,'gz'=2] {'gx','gy','gz'}, use_global_device_ids=true, to_apply=%region_17.0 | all-reduce | flops 96 | bytes 768 | tf_op jit(solution)/shard_map/psum | solution.py:145
  520.8 1.2 multiply_reduce_fusion.2
  522.0 40.5 %psum.31 = f32[3,32]{1,0:T(4,128)S(1)} all-reduce(f32[3,32]{1,0:T(4,128)S(1)} %pad_maximum_fusion.4), channel_id=1, replica_groups=mesh['gx'=4,'gy'=4,'gz'=2] {'gx','gy','gz'}, use_global_device_ids=true, to_apply=%region_22.0 | all-reduce | flops 96 | bytes 768 | tf_op jit(solution)/shard_map/psum | solution.py:145
  562.5 1.1 add_bitcast_fusion
  565.0 27.3 %all-gather.25.cloned.1.call-done = f32[2,32,4096]{2,1,0:T(8,128)} async-done(((f32[2,32,1024]{2,1,0:T(8,128)}), f32[2,32,4096]{2,1,0:T(8,128)}) %all-gather.25.cloned.1.call-update) | async-done | bytes 1048592 | tf_op jit(solution)/shard_map/all_gather | solution.py:167
  592.3 2.2 slice_bitcast_fusion
  (69 shorter events, 10.0 us)
Async XLA Ops:
  7.2 29.4 %all-gather.15.cloned.1.call-start = ((), (), s32[]{:S(2)}) async-start(), calls=%async_computation.10 | async-start | bytes 1179648 | tf_op jit(solution)/shard_map/all_gather | solution.py:125
  9.6 93.2 %reduce-scatter.6.cloned.1.call-start = ((), (), s32[]{:S(2)}) async-start(), calls=%async_computation.5 | async-start | bytes 655360 | tf_op jit(solution)/shard_map/reduce_scatter | solution.py:127
  22.6 2.6 copy-start.6
  36.6 1.2 copy-start
  80.9 46.1 %all-gather.17.cloned.1.call-start = ((), (), s32[]{:S(2)}) async-start(), calls=%async_computation.11 | async-start | bytes 1179648 | tf_op jit(solution)/shard_map/all_gather | solution.py:125
  104.6 88.7 %reduce-scatter.8.cloned.1.call-start = ((), (), s32[]{:S(2)}) async-start(), calls=%async_computation.6 | async-start | bytes 655360 | tf_op jit(solution)/shard_map/reduce_scatter | solution.py:127
  127.0 1.2 copy-start.2
  171.3 45.9 %all-gather.19.cloned.1.call-start = ((), (), s32[]{:S(2)}) async-start(), calls=%async_computation.12 | async-start | bytes 1179648 | tf_op jit(solution)/shard_map/all_gather | solution.py:125
  195.0 106.3 %reduce-scatter.10.cloned.1.call-start = ((), (), s32[]{:S(2)}) async-start(), calls=%async_computation.7 | async-start | bytes 655360 | tf_op jit(solution)/shard_map/reduce_scatter | solution.py:127
  217.1 1.2 copy-start.3
  261.4 65.4 %all-gather.21.cloned.1.call-start = ((), (), s32[]{:S(2)}) async-start(), calls=%async_computation.13 | async-start | bytes 1179648 | tf_op jit(solution)/shard_map/all_gather | solution.py:125
  303.2 107.9 %reduce-scatter.12.cloned.1.call-start = ((), (), s32[]{:S(2)}) async-start(), calls=%async_computation.8 | async-start | bytes 655360 | tf_op jit(solution)/shard_map/reduce_scatter | solution.py:127
  326.9 1.2 copy-start.4
  328.1 83.0 %copy-start.5 = (f32[1,32,1024]{2,1,0:T(8,128)S(1)}, f32[1,32,1024]{2,1,0:T(8,128)}, u32[]{:S(2)}) copy-start(f32[1,32,1024]{2,1,0:T(8,128)} %reduce-scatter.10.cloned.1.call-done) | copy-start | bytes 393220
  371.2 65.5 %all-gather.23.cloned.1.call-start = ((), (), s32[]{:S(2)}) async-start(), calls=%async_computation.14 | async-start | bytes 1179648 | tf_op jit(solution)/shard_map/all_gather | solution.py:125
  413.0 107.8 %reduce-scatter.14.cloned.1.call-start = ((), (), s32[]{:S(2)}) async-start(), calls=%async_computation.9 | async-start | bytes 655360 | tf_op jit(solution)/shard_map/reduce_scatter | solution.py:127
  436.7 1.2 copy-start.1
  481.0 111.3 %all-gather.25.cloned.1.call-start = ((), (), s32[]{:S(2)}) async-start(), calls=%async_computation.15 | async-start | bytes 1310720 | tf_op jit(solution)/shard_map/all_gather | solution.py:167
Sparse Core Ops, SparseCore 0:
  10.4 26.0 all-gather.14
  81.0 21.8 reduce-scatter.5
  105.3 21.6 all-gather.16
  171.4 21.8 reduce-scatter.7
  195.5 21.5 all-gather.18
  261.6 21.8 reduce-scatter.9
  303.3 23.5 all-gather.20
  371.3 21.8 reduce-scatter.11
  413.1 23.5 all-gather.22
  481.1 21.8 reduce-scatter.13
  564.5 27.7 all-gather.24
where the time goes:
time: 602 us; the launch traced here: 601 us
  Pallas kernels  215 us (36%)
  waiting for transfers between devices  173 us (29%)
  blocking collectives  170 us (28%)
  other arithmetic  14.7 us (2%)
  between operations  14.1 us (2%)
  local copies, waits for them, and re-layouts  13.3 us (2%)
    pallas_call x5, Pallas kernels, product(): pl.pallas_call(functools.partial(product_kernel, tile), grid=(cols // ste...  215 us
    psum x4, blocking collectives, on_device(): gamma_now, delta_now, omega_now = lax.psum(sums, ('gx', 'gy', 'gz'))  160 us
    all_gather x5, waiting for transfers between devices, matvec(): gathered = lax.all_gather(vector * scaled_area, PLANE, axis=0)  102 us
    reduce_scatter x5, waiting for transfers between devices, matvec(): summed = lax.psum_scatter(partial_value, 'gx', scatter_dimension=0)  43.2 us
    all_gather x1, waiting for transfers between devices, on_device(): both = lax.all_gather(jnp.stack([solution, residual]), 'gx', axis=2)  27.3 us
  transfers between devices with their start and end apart: 11, of which 8 were waited for; matrix products, arithmetic and copies ran while one was open for 1% of the time, Pallas kernels for 0%

commit v1 on v0

v1 whole, which is shorter than its diff:
```python
import functools

import jax
import jax.numpy as jnp
from jax import lax
from jax.experimental import pallas as pl
from jax.experimental.pallas import tpu as pltpu
from jax.sharding import PartitionSpec as P

ITERS = 4
soft_sq = 0.0025
PLANE = ("gy", "gz")
MESH = pl.DeviceIdType.MESH
NEAR = 2


def three(value):
    high = lax.reduce_precision(value, 8, 7)
    rest = value - high
    mid = lax.reduce_precision(rest, 8, 7)
    return high, mid, lax.reduce_precision(rest - mid, 8, 7)


def features(row_pan, col_pan):
    left, right = [], []
    for axis in range(3):
        r = three(row_pan[axis])
        c = three(-2.0 * col_pan[axis])
        for i in range(3):
            for j in range(3):
                if i + j < 4:
                    left.append(r[i])
                    right.append(c[j])
    r_sq = three(jnp.sum(row_pan[:3] ** 2, 0))
    c_sq = three(jnp.sum(col_pan[:3] ** 2, 0) + soft_sq)
    one_r, one_c = jnp.ones_like(row_pan[0]), jnp.ones_like(col_pan[0])
    for i in range(3):
        left += [r_sq[i], one_r]
        right += [one_c, c_sq[i]]
    left += [jnp.zeros_like(one_r)] * 2
    right += [jnp.zeros_like(one_c)] * 2
    return jnp.stack(left).astype(jnp.bfloat16), jnp.stack(right).astype(jnp.bfloat16)


def flip(index, offset, count):
    result = 0
    bit = 1
    while bit < count:
        a = lax.rem(lax.div(index, bit), 2)
        b = (offset // bit) % 2 if isinstance(offset, int) else lax.rem(lax.div(offset, bit), 2)
        result = result + lax.rem(a + b, 2) * bit
        bit *= 2
    return result


def solve_kernel(
    depth, lines, cores, tile,
    b_ref, start_ref, scaled_ref, area_ref, diag_ref, left_ref, right_ref,
    sol_out, res_out, hist_out,
    vec, sol, res, img, direc, sdir, zdir, prev,
    sent, held, parts, near_sum, chunk, chunk_in, sums, sums_in, sums_mid, sums_mid_in,
    vec_send, vec_recv, chunk_send, chunk_recv,
    one_send, one_recv, two_send, two_recv, out_send, out_recv,
):
    plane = lines * cores
    cases, width = b_ref.shape
    step_cols = min(256, width)
    per = width // step_cols
    gx = lax.axis_index("gx")
    gy = lax.axis_index("gy")
    gz = lax.axis_index("gz")
    mine = gy * cores + gz

    def in_plane(k):
        q = flip(mine, k, plane)
        return (gx, lax.div(q, cores), lax.rem(q, cores))

    def in_line(k):
        return (flip(gx, k, depth), gy, gz)

    barrier = pltpu.get_barrier_semaphore()
    for k in range(1, plane):
        pl.semaphore_signal(barrier, inc=1, device_id=in_plane(k), device_id_type=MESH)
    for k in range(1, depth):
        pl.semaphore_signal(barrier, inc=1, device_id=in_line(k), device_id_type=MESH)
    pl.semaphore_wait(barrier, plane - 1 + depth - 1)

    def vec_copy(par, k):
        return pltpu.make_async_remote_copy(
            src_ref=sent.at[par], dst_ref=held.at[par, k - 1],
            send_sem=vec_send.at[par, k - 1], recv_sem=vec_recv.at[par, k - 1],
            device_id=in_plane(k), device_id_type=MESH)

    def chunk_copy(par, k):
        return pltpu.make_async_remote_copy(
            src_ref=chunk.at[par, k], dst_ref=chunk_in.at[par, k],
            send_sem=chunk_send.at[par, k], recv_sem=chunk_recv.at[par, k],
            device_id=in_line(k), device_id_type=MESH)

    def one_copy(par, k):
        return pltpu.make_async_remote_copy(
            src_ref=sums.at[par], dst_ref=sums_in.at[par, gx],
            send_sem=one_send.at[par, k - 1], recv_sem=one_recv.at[par, k - 1],
            device_id=in_line(k), device_id_type=MESH)

    def two_copy(par, k):
        return pltpu.make_async_remote_copy(
            src_ref=sums_mid.at[par], dst_ref=sums_mid_in.at[par, mine],
            send_sem=two_send.at[par, k - 1], recv_sem=two_recv.at[par, k - 1],
            device_id=in_plane(k), device_id_type=MESH)

    def split(k, value):
        high = value.astype(jnp.bfloat16)
        rest = value - high.astype(jnp.float32)
        mid = rest.astype(jnp.bfloat16)
        parts[k, :cases] = high
        parts[k, cases:2 * cases] = mid
        parts[k, 2 * cases:] = (rest - mid.astype(jnp.float32)).astype(jnp.bfloat16)

    def sweep(blocks, col):
        right = right_ref[:, pl.ds(col, step_cols)]
        full = jnp.zeros((3 * cases, step_cols), jnp.float32)
        low_sum = jnp.zeros((cases, step_cols), jnp.float32)
        for k in blocks:
            base = flip(mine, k, plane) * width
            for sub in range(width // tile):
                left = left_ref[pl.ds(pl.multiple_of(base + sub * tile, tile), tile), :]
                value = lax.rsqrt(jnp.dot(left, right, preferred_element_type=jnp.float32))
                high = value.astype(jnp.bfloat16)
                low = (value - high.astype(jnp.float32)).astype(jnp.bfloat16)
                x_all = parts[k, :, sub * tile:(sub + 1) * tile]
                full = full + jnp.dot(x_all, high, preferred_element_type=jnp.float32)
                low_sum = low_sum + jnp.dot(x_all[:cases], low, preferred_element_type=jnp.float32)
        return full[:cases] + (full[cases:2 * cases] + (full[2 * cases:] + low_sum))

    def sums_start_one(par):
        lane = lax.broadcasted_iota(jnp.int32, (cases, 128), 1)
        r, w = res[...], img[...]
        gamma = jnp.sum(r * r, 1, keepdims=True)
        delta = jnp.sum(w * r, 1, keepdims=True)
        omega = jnp.sum(w * w, 1, keepdims=True)
        packed = jnp.where(lane == 0, gamma, jnp.where(lane == 1, delta, omega))
        sums[par] = packed
        sums_in[par, gx] = packed
        for k in range(1, depth):
            one_copy(par, k).start()

    def sums_start_two(par):
        for k in range(1, depth):
            one_copy(par, k).wait()
        total = sums_in[par, 0]
        for g in range(1, depth):
            total = total + sums_in[par, g]
        sums_mid[par] = total
        sums_mid_in[par, mine] = total
        for k in range(1, plane):
            two_copy(par, k).start()

    def sums_finish(par):
        for k in range(1, plane):
            two_copy(par, k).wait()
        total = sums_mid_in[par, 0]
        for q in range(1, plane):
            total = total + sums_mid_in[par, q]
        return total

    def factors(total, turn):
        gamma, delta, omega = total[:, 0:1], total[:, 1:2], total[:, 2:3]
        lane = lax.broadcasted_iota(jnp.int32, (cases, 128), 1)
        hist_out[...] = jnp.where(lane == turn, jnp.sqrt(omega / gamma), hist_out[...])
        first = turn == 0
        beta = jnp.where(first, 0.0, gamma / prev[:, 0:1])
        alpha = gamma / jnp.where(first, delta, delta - beta * gamma / prev[:, 1:2])
        prev[...] = jnp.where(lane == 0, gamma, alpha)
        return alpha, beta

    def advance(alpha, beta):
        sdir[...] = img[...] + beta * sdir[...]
        direc[...] = res[...] + beta * direc[...]
        sol[...] = sol[...] + alpha * direc[...]
        res[...] = res[...] - alpha * sdir[...]

    zero = jnp.zeros((cases, width), jnp.float32)
    sol[...] = start_ref[...]
    vec[...] = start_ref[...]
    res[...] = zero
    img[...] = zero
    direc[...] = zero
    sdir[...] = zero
    zdir[...] = zero
    prev[...] = jnp.ones_like(prev)
    hist_out[...] = jnp.zeros_like(hist_out)

    def step(turn, carry):
        par = lax.rem(turn, 2)
        scaled = vec[...] * scaled_ref[...]
        sent[par] = scaled
        for k in range(1, plane):
            vec_copy(par, k).start()
        sums_start_one(par)
        split(0, scaled)
        for k in range(1, NEAR):
            vec_copy(par, k).wait_recv()
            split(k, held[par, k - 1])

        def near(j, carry):
            col = pl.multiple_of(j * step_cols, step_cols)
            near_sum[:, pl.ds(col, step_cols)] = sweep(range(NEAR), col)
            return carry

        lax.fori_loop(0, depth * per, near, 0)
        for k in range(NEAR, plane):
            vec_copy(par, k).wait_recv()
            split(k, held[par, k - 1])
        sums_start_two(par)

        def far(j, carry):
            k = depth - 1 - lax.div(j, per)
            inner = pl.multiple_of(lax.rem(j, per) * step_cols, step_cols)
            col = pl.multiple_of(flip(gx, k, depth) * width + inner, step_cols)
            got = sweep(range(NEAR, plane), col) + near_sum[:, pl.ds(col, step_cols)]
            chunk[par, k, :, pl.ds(inner, step_cols)] = got

            @pl.when(jnp.logical_and(lax.rem(j, per) == per - 1, k > 0))
            def _():
                chunk_copy(par, k).start()
            return carry

        lax.fori_loop(0, depth * per, far, 0)
        total = sums_finish(par)
        summed = chunk[par, 0]
        for k in range(depth - 1, 0, -1):
            chunk_copy(par, k).wait()
            summed = summed + chunk_in[par, k]
        for k in range(1, plane):
            vec_copy(par, k).wait_send()
        image = diag_ref[...] * vec[...] + area_ref[...] * summed

        @pl.when(turn == 0)
        def _():
            res[...] = b_ref[...] - image
            vec[...] = res[...]

        @pl.when(turn == 1)
        def _():
            img[...] = image
            vec[...] = image

        @pl.when(turn > 1)
        def _():
            alpha, beta = factors(total, turn - 2)
            advance(alpha, beta)
            zdir[...] = image + beta * zdir[...]
            img[...] = img[...] - alpha * zdir[...]
            vec[...] = img[...]

        return carry

    turns = ITERS + 1
    lax.fori_loop(0, turns, step, 0)
    par = turns % 2
    sums_start_one(par)
    sums_start_two(par)
    alpha, beta = factors(sums_finish(par), ITERS - 1)
    advance(alpha, beta)

    spot = pl.ds(pl.multiple_of(gx * width, width), width)

    def out_copy(which, src, dst, k):
        return pltpu.make_async_remote_copy(
            src_ref=src, dst_ref=dst.at[:, spot],
            send_sem=out_send.at[which, k - 1], recv_sem=out_recv.at[which, k - 1],
            device_id=in_line(k), device_id_type=MESH)

    for k in range(1, depth):
        out_copy(0, sol, sol_out, k).start()
        out_copy(1, res, res_out, k).start()
    sol_out[:, spot] = sol[...]
    res_out[:, spot] = res[...]
    for k in range(1, depth):
        out_copy(0, sol, sol_out, k).wait()
        out_copy(1, res, res_out, k).wait()


def solve(b_own, start, scaled, area, diag, left, right, depth, lines, cores):
    cases, width = b_own.shape
    plane = lines * cores
    cols = right.shape[1]
    tile = min(256, width)
    f32 = jnp.float32
    state = pltpu.VMEM((cases, width), f32)
    dma = pltpu.SemaphoreType.DMA
    whole = pl.BlockSpec(memory_space=pltpu.VMEM)
    return pl.pallas_call(
        functools.partial(solve_kernel, depth, lines, cores, tile),
        out_shape=(
            jax.ShapeDtypeStruct((cases, cols), f32),
            jax.ShapeDtypeStruct((cases, cols), f32),
            jax.ShapeDtypeStruct((cases, 128), f32),
        ),
        in_specs=[whole] * 7,
        out_specs=(whole,) * 3,
        scratch_shapes=[state] * 7 + [
            pltpu.VMEM((cases, 128), f32),
            pltpu.VMEM((2, cases, width), f32),
            pltpu.VMEM((2, plane - 1, cases, width), f32),
            pltpu.VMEM((plane, 3 * cases, width), jnp.bfloat16),
            pltpu.VMEM((cases, cols), f32),
            pltpu.VMEM((2, depth, cases, width), f32),
            pltpu.VMEM((2, depth, cases, width), f32),
            pltpu.VMEM((2, cases, 128), f32),
            pltpu.VMEM((2, depth, cases, 128), f32),
            pltpu.VMEM((2, cases, 128), f32),
            pltpu.VMEM((2, plane, cases, 128), f32),
            dma((2, plane - 1)), dma((2, plane - 1)),
            dma((2, depth)), dma((2, depth)),
            dma((2, depth - 1)), dma((2, depth - 1)),
            dma((2, plane - 1)), dma((2, plane - 1)),
            dma((2, depth - 1)), dma((2, depth - 1)),
        ],
        compiler_params=pltpu.CompilerParams(
            collective_id=0, has_side_effects=True, vmem_limit_bytes=48 * 1024 * 1024),
    )(b_own, start, scaled, area, diag, left, right)


def on_device(panels, diagonal, right_side, start_guess):
    col_count = panels.shape[1]
    depth = lax.axis_size("gx")
    lines = lax.axis_size("gy")
    cores = lax.axis_size("gz")
    total = col_count * lines * cores
    width = col_count // depth
    mine = lax.axis_index("gx") * width

    def own(value):
        return lax.dynamic_slice_in_dim(value, mine, width, value.ndim - 1)

    pan_own = own(panels)
    diag_own = own(diagonal)[None, :]
    area_own = pan_own[3][None, :]
    scaled_area = area_own * total ** (-0.5)
    row_pan = lax.all_gather(pan_own, PLANE, axis=0)
    row_pan = jnp.swapaxes(row_pan, 0, 1).reshape(4, -1)
    left, right = features(row_pan, panels)
    solution, residual, records = solve(
        own(right_side), own(start_guess), scaled_area, area_own, diag_own,
        left.T, right, depth, lines, cores)
    return solution, residual, records[:, :ITERS].T


def solution(mesh):
    placed = (P(None, PLANE), P(PLANE), P(None, PLANE), P(None, PLANE))
    return jax.shard_map(
        on_device,
        mesh=mesh,
        in_specs=placed,
        out_specs=(P(None, PLANE), P(None, PLANE), P()),
        check_vma=False,
    )
```

time: 602 us -> 307 us (0.51)
  waiting for transfers between devices: 173 us -> 0 us
  blocking collectives: 170 us -> 10.7 us
  Pallas kernels: 215 us -> 281 us
  between operations: 14.1 us -> 0.78 us
  other arithmetic: 14.7 us -> 2.22 us
    psum x4 -> x0, blocking collectives: 160 us -> none  [on_device(): gamma_now, delta_now, omega_now = lax.psum(sums, ('gx', 'gy', 'gz'))]
    all_gather x6 -> x0, waiting for transfers between devices: 129 us -> none  [the longest x5 102 us: matvec(): gathered = lax.all_gather(vector * scaled_area, PLANE, axis=0)]
    pallas_call x5 -> x1, Pallas kernels: 215 us -> 281 us  [solve(): pl.pallas_call(functools.partial(solve_kernel, depth, lines, cores, tile)...]
    reduce_scatter x5 -> x0, waiting for transfers between devices: 43.2 us -> none  [matvec(): summed = lax.psum_scatter(partial_value, 'gx', scatter_dimension=0)]
  transfers between devices with their start and end apart: 11 -> 0, of which waited for: 8 -> 0; matrix products, arithmetic and copies ran while one was open for 1% -> 0% of each run, Pallas kernels for 0% -> 0%
where the time goes in v1:
time: 307 us; the launch traced here: 305 us
  Pallas kernels  281 us (92%)
  blocking collectives  10.7 us (3%)
  local copies, waits for them, and re-layouts  10 us (3%)
    pallas_call x1, Pallas kernels, solve(): pl.pallas_call(functools.partial(solve_kernel, depth, lines, cores, tile)...  281 us
    all_gather x1, blocking collectives, on_device(): row_pan = lax.all_gather(pan_own, PLANE, axis=0)  10.7 us

profile of v1, /device:TPU:0, one launch (start us, length us, event | category | flops | bytes accessed | tf_op | source)
XLA Modules:
  0.0 304.5 jit_solution(3281410501540819625)
XLA Ops:
  0.6 0.0 copy-start.1
  0.6 0.7 dynamic_slice.15
  1.4 0.8 broadcast_multiply_fusion
  2.2 0.7 dynamic-slice_bitcast_fusion
  2.9 0.9 multiply_reduce_fusion
  3.8 10.7 %all-gather.1 = f32[8,4,1024]{2,1,0:T(4,128)S(1)} all-gather(f32[1,4,1024]{2,1,0:T(4,128)S(1)} %dynamic-slice_bitcast_fusion), channel_id=2, replica_groups=mesh['gx'=4,'gy'=4,'gz'=2] {'gy','gz'}, dimensions={0}, use_global_device_ids=true | all-gather | bytes 147456 | tf_op jit(solution)/shard_map/all_gather | solution.py:342
  14.5 0.1 fusion
  14.6 0.1 fusion.17
  14.7 0.1 fusion.6
  14.9 0.1 fusion.2
  15.1 1.5 stack.11
  16.6 0.0 copy-done.1
  16.6 0.1 fusion.14
  16.8 0.8 stack.13.right_ref
  17.6 1.0 constant_dynamic-slice_fusion
  18.6 1.0 copy.17
  19.6 280.8 %shard_map.67 = (f32[32,4096]{1,0:T(8,128)S(1)}, f32[32,4096]{1,0:T(8,128)S(1)}, f32[32,128]{1,0:T(8,128)S(1)}) custom-call(f32[32,1024]{1,0:T(8,128)S(1)} %get-tuple-element.48.b_ref, f32[32,1024]{1,0:T(8,128)S(1)} %get-tuple-element.47.start_ref, f32[1,1024]{1,0:T(1,128)S(1)} %get-tuple-element.18.scaled_ref, f32[1,1024]{1,0:T(1,128)S(1)} %get-tuple-element.19.area_ref, ...), custom_call_target="tpu_custom_call" | custom-call | tf_op jit(solution)/shard_map/pallas_call | solution.py:294
  300.4 0.0 copy-start
  300.4 0.8 copy-done
  301.2 0.7 copy.18
  301.9 1.9 copy.22
  303.7 0.8 copy.23
  (8 shorter events, 0.1 us)
Async XLA Ops:
  0.6 16.0 %copy-start.1 = (f32[4,4096]{1,0:T(4,128)S(1)}, f32[4,4096]{1,0:T(4,128)}, u32[]{:S(2)}) copy-start(f32[4,4096]{1,0:T(4,128)} %param.4) | copy-start | bytes 196612
  300.4 0.8 copy-start

commit v2 on v1

--- a/solution.py
+++ b/solution.py
@@ -12,6 +12,9 @@
 PLANE = ("gy", "gz")
 MESH = pl.DeviceIdType.MESH
 NEAR = 2
+UNIT = 512
+STEP = 512
+CACHE_BYTES = 48 * 1024 * 1024
 
 
 def three(value):
@@ -54,22 +57,24 @@
 
 
 def solve_kernel(
-    depth, lines, cores, tile,
+    depth, lines, cores, tile, unit, step_cols, kept,
     b_ref, start_ref, scaled_ref, area_ref, diag_ref, left_ref, right_ref,
-    sol_out, res_out, hist_out,
-    vec, sol, res, img, direc, sdir, zdir, prev,
-    sent, held, parts, near_sum, chunk, chunk_in, sums, sums_in, sums_mid, sums_mid_in,
+    sol, res, hist_out,
+    vec, zdir, prev, direc, sdir, wide,
+    sent, held, parts, chunk, chunk_in, sums, sums_in, sums_mid, sums_mid_in,
+    slot_high, slot_low, kept_high, kept_low,
     vec_send, vec_recv, chunk_send, chunk_recv,
-    one_send, one_recv, two_send, two_recv, out_send, out_recv,
+    one_send, one_recv, two_send, two_recv, wide_send, wide_recv, start_sem,
 ):
     plane = lines * cores
     cases, width = b_ref.shape
-    step_cols = min(256, width)
+    halves = width // unit
     per = width // step_cols
     gx = lax.axis_index("gx")
     gy = lax.axis_index("gy")
     gz = lax.axis_index("gz")
     mine = gy * cores + gz
+    spot = pl.ds(pl.multiple_of(gx * width, width), width)
 
     def in_plane(k):
         q = flip(mine, k, plane)
@@ -85,15 +90,26 @@
         pl.semaphore_signal(barrier, inc=1, device_id=in_line(k), device_id_type=MESH)
     pl.semaphore_wait(barrier, plane - 1 + depth - 1)
 
+    def relayed(k):
+        return k >= cores and k % cores > 0
+
     def vec_copy(par, k):
+        hand = k % cores
         return pltpu.make_async_remote_copy(
-            src_ref=sent.at[par], dst_ref=held.at[par, k - 1],
+            src_ref=held.at[par, k - hand - 1] if relayed(k) else sent.at[par],
+            dst_ref=held.at[par, k - 1],
             send_sem=vec_send.at[par, k - 1], recv_sem=vec_recv.at[par, k - 1],
-            device_id=in_plane(k), device_id_type=MESH)
+            device_id=in_plane(hand if relayed(k) else k), device_id_type=MESH)
+
+    def wide_copy(par, k):
+        return pltpu.make_async_remote_copy(
+            src_ref=vec, dst_ref=wide.at[par, gx],
+            send_sem=wide_send.at[par, k - 1], recv_sem=wide_recv.at[par, k - 1],
+            device_id=in_line(k), device_id_type=MESH)
 
     def chunk_copy(par, k):
         return pltpu.make_async_remote_copy(
-            src_ref=chunk.at[par, k], dst_ref=chunk_in.at[par, k],
+            src_ref=chunk.at[par, k], dst_ref=chunk_in.at[par, k - 1],
             send_sem=chunk_send.at[par, k], recv_sem=chunk_recv.at[par, k],
             device_id=in_line(k), device_id_type=MESH)
 
@@ -117,25 +133,47 @@
         parts[k, cases:2 * cases] = mid
         parts[k, 2 * cases:] = (rest - mid.astype(jnp.float32)).astype(jnp.bfloat16)
 
-    def sweep(blocks, col):
+    def build(high_ref, low_ref, k, half, col):
         right = right_ref[:, pl.ds(col, step_cols)]
-        full = jnp.zeros((3 * cases, step_cols), jnp.float32)
-        low_sum = jnp.zeros((cases, step_cols), jnp.float32)
-        for k in blocks:
-            base = flip(mine, k, plane) * width
-            for sub in range(width // tile):
-                left = left_ref[pl.ds(pl.multiple_of(base + sub * tile, tile), tile), :]
-                value = lax.rsqrt(jnp.dot(left, right, preferred_element_type=jnp.float32))
-                high = value.astype(jnp.bfloat16)
-                low = (value - high.astype(jnp.float32)).astype(jnp.bfloat16)
-                x_all = parts[k, :, sub * tile:(sub + 1) * tile]
-                full = full + jnp.dot(x_all, high, preferred_element_type=jnp.float32)
-                low_sum = low_sum + jnp.dot(x_all[:cases], low, preferred_element_type=jnp.float32)
+        base = flip(mine, k, plane) * width + half * unit
+        for sub in range(unit // tile):
+            left = left_ref[:, pl.ds(pl.multiple_of(base + sub * tile, tile), tile)]
+            value = lax.rsqrt(lax.dot_general(
+                left, right, (((0,), (0,)), ((), ())), preferred_element_type=jnp.float32))
+            high = value.astype(jnp.bfloat16)
+            high_ref[sub * tile:(sub + 1) * tile, :] = high
+            low_ref[sub * tile:(sub + 1) * tile, :] = (
+                value - high.astype(jnp.float32)).astype(jnp.bfloat16)
+
+    def apply(sums, high_ref, low_ref, k, half):
+        full, low_sum = sums
+        x_all = parts[k, :, half * unit:(half + 1) * unit]
+        full = full + jnp.dot(x_all, high_ref[...], preferred_element_type=jnp.float32)
+        low_sum = low_sum + jnp.dot(
+            x_all[:cases], low_ref[...], preferred_element_type=jnp.float32)
+        return full, low_sum
+
+    def empty():
+        return (jnp.zeros((3 * cases, step_cols), jnp.float32),
+                jnp.zeros((cases, step_cols), jnp.float32))
+
+    def joined(sums):
+        full, low_sum = sums
         return full[:cases] + (full[cases:2 * cases] + (full[2 * cases:] + low_sum))
+
+    def build_slot(i, who, col):
+        build(slot_high[i % 2], slot_low[i % 2], *who, col)
+
+    def apply_slot(sums, i, who):
+        return apply(sums, slot_high[i % 2], slot_low[i % 2], *who)
+
+    def kept_at(c, j, half):
+        rows = pl.ds(half * unit, unit)
+        return kept_high.at[c, j, rows], kept_low.at[c, j, rows]
 
     def sums_start_one(par):
         lane = lax.broadcasted_iota(jnp.int32, (cases, 128), 1)
-        r, w = res[...], img[...]
+        r, w = res[:, spot], vec[...]
         gamma = jnp.sum(r * r, 1, keepdims=True)
         delta = jnp.sum(w * r, 1, keepdims=True)
         omega = jnp.sum(w * w, 1, keepdims=True)
@@ -174,20 +212,33 @@
         prev[...] = jnp.where(lane == 0, gamma, alpha)
         return alpha, beta
 
-    def advance(alpha, beta):
-        sdir[...] = img[...] + beta * sdir[...]
-        direc[...] = res[...] + beta * direc[...]
-        sol[...] = sol[...] + alpha * direc[...]
-        res[...] = res[...] - alpha * sdir[...]
-
-    zero = jnp.zeros((cases, width), jnp.float32)
-    sol[...] = start_ref[...]
-    vec[...] = start_ref[...]
-    res[...] = zero
-    img[...] = zero
-    direc[...] = zero
-    sdir[...] = zero
-    zdir[...] = zero
+    def wide_start(par):
+        wide[par, gx] = vec[...]
+        for k in range(1, depth):
+            wide_copy(par, k).start()
+
+    def wide_finish(par):
+        for k in range(1, depth):
+            wide_copy(par, k).wait()
+
+    def advance(par, alpha, beta):
+        for g in range(depth):
+            cols = slice(g * width, (g + 1) * width)
+            turned = wide[par, g] + beta * sdir[g]
+            ahead = res[:, cols] + beta * direc[g]
+            sdir[g] = turned
+            direc[g] = ahead
+            sol[:, cols] = sol[:, cols] + alpha * ahead
+            res[:, cols] = res[:, cols] - alpha * turned
+
+    fetch = pltpu.make_async_copy(start_ref, sol, start_sem)
+    fetch.start()
+    fetch.wait()
+    vec[...] = sol[:, spot]
+    res[...] = jnp.zeros_like(res)
+    direc[...] = jnp.zeros_like(direc)
+    sdir[...] = jnp.zeros_like(sdir)
+    zdir[...] = jnp.zeros_like(zdir)
     prev[...] = jnp.ones_like(prev)
     hist_out[...] = jnp.zeros_like(hist_out)
 
@@ -196,63 +247,111 @@
         scaled = vec[...] * scaled_ref[...]
         sent[par] = scaled
         for k in range(1, plane):
-            vec_copy(par, k).start()
+            if not relayed(k):
+                vec_copy(par, k).start()
         sums_start_one(par)
+        wide_start(par)
         split(0, scaled)
         for k in range(1, NEAR):
             vec_copy(par, k).wait_recv()
             split(k, held[par, k - 1])
 
-        def near(j, carry):
-            col = pl.multiple_of(j * step_cols, step_cols)
-            near_sum[:, pl.ds(col, step_cols)] = sweep(range(NEAR), col)
-            return carry
-
-        lax.fori_loop(0, depth * per, near, 0)
-        for k in range(NEAR, plane):
-            vec_copy(par, k).wait_recv()
-            split(k, held[par, k - 1])
-        sums_start_two(par)
-
-        def far(j, carry):
+        count = depth * per
+        first = [(k, h) for k in range(NEAR) for h in range(halves)]
+        fresh = [(k, h) for k in range(NEAR + kept, plane) for h in range(halves)]
+        known = [(c, h) for c in range(kept) for h in range(halves)]
+
+        def place(j):
             k = depth - 1 - lax.div(j, per)
             inner = pl.multiple_of(lax.rem(j, per) * step_cols, step_cols)
             col = pl.multiple_of(flip(gx, k, depth) * width + inner, step_cols)
-            got = sweep(range(NEAR, plane), col) + near_sum[:, pl.ds(col, step_cols)]
-            chunk[par, k, :, pl.ds(inner, step_cols)] = got
+            return k, inner, col
+
+        def next_col(j):
+            return place(lax.rem(j + 1, count))[2]
+
+        def rolled(sums, units, j, col, extra):
+            done = 0
+            for i, who in enumerate(units):
+                last = i == len(units) - 1
+                build_slot(i + 1, units[0 if last else i + 1], next_col(j) if last else col)
+                sums = apply_slot(sums, i, who)
+                upto = len(extra) * (i + 1) // len(units)
+                for c, h in extra[done:upto]:
+                    sums = apply(sums, *kept_at(c, j, h), NEAR + c, h)
+                done = upto
+            for c, h in extra[done:]:
+                sums = apply(sums, *kept_at(c, j, h), NEAR + c, h)
+            return sums
+
+        def near(j, carry):
+            k, inner, col = place(j)
+            chunk[par, k, :, pl.ds(inner, step_cols)] = joined(rolled(empty(), first, j, col, []))
+            return carry
+
+        build_slot(0, first[0], place(0)[2])
+        split_at = count * 3 // 4
+        lax.fori_loop(0, split_at, near, 0)
+        for k in range(cores, plane, cores):
+            vec_copy(par, k).wait_recv()
+            for hand in range(1, cores):
+                vec_copy(par, k + hand).start()
+        for k in range(cores, plane, cores):
+            split(k, held[par, k - 1])
+        lax.fori_loop(split_at, count, near, 0)
+        for k in range(NEAR, plane):
+            if k % cores:
+                vec_copy(par, k).wait_recv()
+                split(k, held[par, k - 1])
+        sums_start_two(par)
+
+        if fresh:
+            build_slot(0, fresh[0], place(0)[2])
+
+        def far(j, carry):
+            k, inner, col = place(j)
+
+            @pl.when(turn == 0)
+            def _():
+                for c, h in known:
+                    build(*kept_at(c, j, h), NEAR + c, h, col)
+
+            chunk[par, k, :, pl.ds(inner, step_cols)] += joined(
+                rolled(empty(), fresh, j, col, known))
 
             @pl.when(jnp.logical_and(lax.rem(j, per) == per - 1, k > 0))
             def _():
                 chunk_copy(par, k).start()
             return carry
 
-        lax.fori_loop(0, depth * per, far, 0)
+        lax.fori_loop(0, count, far, 0)
         total = sums_finish(par)
         summed = chunk[par, 0]
         for k in range(depth - 1, 0, -1):
             chunk_copy(par, k).wait()
-            summed = summed + chunk_in[par, k]
+            summed = summed + chunk_in[par, k - 1]
         for k in range(1, plane):
             vec_copy(par, k).wait_send()
+        wide_finish(par)
         image = diag_ref[...] * vec[...] + area_ref[...] * summed
 
         @pl.when(turn == 0)
         def _():
-            res[...] = b_ref[...] - image
-            vec[...] = res[...]
+            vec[...] = b_ref[...] - image
 
         @pl.when(turn == 1)
         def _():
-            img[...] = image
+            for g in range(depth):
+                res[:, g * width:(g + 1) * width] = wide[par, g]
             vec[...] = image
 
         @pl.when(turn > 1)
         def _():
             alpha, beta = factors(total, turn - 2)
-            advance(alpha, beta)
-            zdir[...] = image + beta * zdir[...]
-            img[...] = img[...] - alpha * zdir[...]
-            vec[...] = img[...]
+            advance(par, alpha, beta)
+            turned = image + beta * zdir[...]
+            zdir[...] = turned
+            vec[...] = vec[...] - alpha * turned
 
         return carry
 
@@ -260,26 +359,11 @@
     lax.fori_loop(0, turns, step, 0)
     par = turns % 2
     sums_start_one(par)
+    wide_start(par)
     sums_start_two(par)
     alpha, beta = factors(sums_finish(par), ITERS - 1)
-    advance(alpha, beta)
-
-    spot = pl.ds(pl.multiple_of(gx * width, width), width)
-
-    def out_copy(which, src, dst, k):
-        return pltpu.make_async_remote_copy(
-            src_ref=src, dst_ref=dst.at[:, spot],
-            send_sem=out_send.at[which, k - 1], recv_sem=out_recv.at[which, k - 1],
-            device_id=in_line(k), device_id_type=MESH)
-
-    for k in range(1, depth):
-        out_copy(0, sol, sol_out, k).start()
-        out_copy(1, res, res_out, k).start()
-    sol_out[:, spot] = sol[...]
-    res_out[:, spot] = res[...]
-    for k in range(1, depth):
-        out_copy(0, sol, sol_out, k).wait()
-        out_copy(1, res, res_out, k).wait()
+    wide_finish(par)
+    advance(par, alpha, beta)
 
 
 def solve(b_own, start, scaled, area, diag, left, right, depth, lines, cores):
@@ -287,39 +371,47 @@
     plane = lines * cores
     cols = right.shape[1]
     tile = min(256, width)
+    unit = min(UNIT, width)
+    step_cols = min(STEP, width)
+    kept = min(plane - NEAR, CACHE_BYTES // (4 * width * cols))
+    kept -= (plane - NEAR - kept) * (width // unit) % 2
     f32 = jnp.float32
+    square = pltpu.VMEM((unit, step_cols), jnp.bfloat16)
+    store = pltpu.VMEM((kept, cols // step_cols, width, step_cols), jnp.bfloat16)
     state = pltpu.VMEM((cases, width), f32)
     dma = pltpu.SemaphoreType.DMA
     whole = pl.BlockSpec(memory_space=pltpu.VMEM)
     return pl.pallas_call(
-        functools.partial(solve_kernel, depth, lines, cores, tile),
+        functools.partial(solve_kernel, depth, lines, cores, tile, unit, step_cols, kept),
         out_shape=(
             jax.ShapeDtypeStruct((cases, cols), f32),
             jax.ShapeDtypeStruct((cases, cols), f32),
             jax.ShapeDtypeStruct((cases, 128), f32),
         ),
-        in_specs=[whole] * 7,
+        in_specs=[whole, pl.BlockSpec(memory_space=pl.ANY)] + [whole] * 5,
         out_specs=(whole,) * 3,
-        scratch_shapes=[state] * 7 + [
-            pltpu.VMEM((cases, 128), f32),
+        scratch_shapes=[
+            state, state, pltpu.VMEM((cases, 128), f32),
+            pltpu.VMEM((depth, cases, width), f32), pltpu.VMEM((depth, cases, width), f32),
+            pltpu.VMEM((2, depth, cases, width), f32),
             pltpu.VMEM((2, cases, width), f32),
             pltpu.VMEM((2, plane - 1, cases, width), f32),
             pltpu.VMEM((plane, 3 * cases, width), jnp.bfloat16),
-            pltpu.VMEM((cases, cols), f32),
             pltpu.VMEM((2, depth, cases, width), f32),
-            pltpu.VMEM((2, depth, cases, width), f32),
+            pltpu.VMEM((2, depth - 1, cases, width), f32),
             pltpu.VMEM((2, cases, 128), f32),
             pltpu.VMEM((2, depth, cases, 128), f32),
             pltpu.VMEM((2, cases, 128), f32),
             pltpu.VMEM((2, plane, cases, 128), f32),
+            [square] * 2, [square] * 2, store, store,
             dma((2, plane - 1)), dma((2, plane - 1)),
             dma((2, depth)), dma((2, depth)),
             dma((2, depth - 1)), dma((2, depth - 1)),
             dma((2, plane - 1)), dma((2, plane - 1)),
-            dma((2, depth - 1)), dma((2, depth - 1)),
+            dma((2, depth - 1)), dma((2, depth - 1)), dma(()),
         ],
         compiler_params=pltpu.CompilerParams(
-            collective_id=0, has_side_effects=True, vmem_limit_bytes=48 * 1024 * 1024),
+            collective_id=0, has_side_effects=True, vmem_limit_bytes=67043328),
     )(b_own, start, scaled, area, diag, left, right)
 
 
@@ -343,8 +435,8 @@
     row_pan = jnp.swapaxes(row_pan, 0, 1).reshape(4, -1)
     left, right = features(row_pan, panels)
     solution, residual, records = solve(
-        own(right_side), own(start_guess), scaled_area, area_own, diag_own,
-        left.T, right, depth, lines, cores)
+        own(right_side), start_guess, scaled_area, area_own, diag_own,
+        left, right, depth, lines, cores)
     return solution, residual, records[:, :ITERS].T
 
 

time: 307 us -> 242 us (0.79)
  Pallas kernels: 281 us -> 213 us
  local copies, waits for them, and re-layouts: 10 us -> 15.2 us
    pallas_call x1, Pallas kernels: 281 us -> 213 us  [solve(): pl.pallas_call(functools.partial(solve_kernel, depth, lines, cores, tile,...]
where the time goes in v2:
time: 242 us
  Pallas kernels  213 us (88%)
  local copies, waits for them, and re-layouts  15.2 us (6%)
  blocking collectives  10.7 us (4%)
    pallas_call x1, Pallas kernels, solve(): pl.pallas_call(functools.partial(solve_kernel, depth, lines, cores, tile,...  213 us
    all_gather x1, blocking collectives, on_device(): row_pan = lax.all_gather(pan_own, PLANE, axis=0)  10.7 us

profile of v2, /device:TPU:0, one launch (start us, length us, event | category | flops | bytes accessed | tf_op | source)
XLA Modules:
  0.0 241.7 jit_solution(9674535899411133665)
XLA Ops:
  0.6 0.0 copy-start.1
  0.6 1.3 dynamic_slice.11
  2.0 1.4 broadcast_multiply_fusion
  3.3 0.7 dynamic-slice_bitcast_fusion
  4.1 0.0 copy-done.1
  4.2 10.7 %all-gather.1 = f32[8,4,1024]{2,1,0:T(4,128)S(1)} all-gather(f32[1,4,1024]{2,1,0:T(4,128)S(1)} %dynamic-slice_bitcast_fusion), channel_id=2, replica_groups=mesh['gx'=4,'gy'=4,'gz'=2] {'gy','gz'}, dimensions={0}, use_global_device_ids=true | all-gather | bytes 147456 | tf_op jit(solution)/shard_map/all_gather | solution.py:434
  14.9 0.1 fusion
  15.0 0.1 fusion.17
  15.1 1.6 constant_dynamic-slice_fusion.b_ref
  16.6 0.1 fusion.6
  16.8 0.1 fusion.2
  17.0 4.1 %stack.11.left_ref = bf16[32,8192]{1,0:T(8,128)(2,1)} concatenate(bf16[1,8192]{1,0:T(2,128)(2,1)S(1)} %get-tuple-element.40, bf16[1,8192]{1,0:T(2,128)(2,1)S(1)} %get-tuple-element.40, bf16[1,8192]{1,0:T(2,128)(2,1)S(1)} %get-tuple-element.40, bf16[1,8192]{1,0:T(2,128)(2,1)S(1)} %get-tuple-element.39, bf16[1,8192]{1,0:T(2,128)(2,1)S(1)} %get-tuple-element.39, ...), dimensions={0} | concatenate | bytes 1048576 | tf_op jit(solution)/shard_map/stack | solution.py:45
  21.1 0.1 fusion.14
  21.3 3.3 %stack.13.right_ref = bf16[32,4096]{1,0:T(8,128)(2,1)} concatenate(bf16[1,4096]{1,0:T(2,128)(2,1)S(1)} %get-tuple-element.27, bf16[1,4096]{1,0:T(2,128)(2,1)S(1)} %get-tuple-element.25, bf16[1,4096]{1,0:T(2,128)(2,1)S(1)} %get-tuple-element.22, bf16[1,4096]{1,0:T(2,128)(2,1)S(1)} %get-tuple-element.27, bf16[1,4096]{1,0:T(2,128)(2,1)S(1)} %get-tuple-element.25, ...), dimensions={0} | concatenate | bytes 524288 | tf_op jit(solution)/shard_map/stack | solution.py:45
  24.5 213.1 %shard_map.67 = (f32[32,4096]{1,0:T(8,128)}, f32[32,4096]{1,0:T(8,128)}, f32[32,128]{1,0:T(8,128)}) custom-call(f32[32,1024]{1,0:T(8,128)} %constant_dynamic-slice_fusion.b_ref, f32[32,4096]{1,0:T(8,128)} %start_ref.1, f32[1,1024]{1,0:T(1,128)} %get-tuple-element.15.scaled_ref, f32[1,1024]{1,0:T(1,128)} %get-tuple-element.16.area_ref, f32[1,1024]{1,0:T(1,128)} %bitcast.21, ...), custom_call_target="tpu_custom_call" | custom-call | tf_op jit(solution)/shard_map/pallas_call | solution.py:384
  237.6 0.7 slice_bitcast_fusion
  238.4 0.7 copy.8
  239.0 0.0 copy-start
  239.0 1.9 copy.12
  241.0 0.0 copy-done
  241.0 0.8 copy.13
  (8 shorter events, 0.2 us)
Async XLA Ops:
  0.6 3.4 %copy-start.1 = (f32[4,4096]{1,0:T(4,128)S(1)}, f32[4,4096]{1,0:T(4,128)}, u32[]{:S(2)}) copy-start(f32[4,4096]{1,0:T(4,128)} %param.4) | copy-start | bytes 196612
  239.0 1.9 copy-start

commit v3 on v2

--- a/solution.py
+++ b/solution.py
@@ -18,31 +18,26 @@
 
 
 def three(value):
-    high = lax.reduce_precision(value, 8, 7)
+    high = value.astype(jnp.bfloat16).astype(jnp.float32)
     rest = value - high
-    mid = lax.reduce_precision(rest, 8, 7)
-    return high, mid, lax.reduce_precision(rest - mid, 8, 7)
-
-
-def features(row_pan, col_pan):
-    left, right = [], []
+    mid = rest.astype(jnp.bfloat16).astype(jnp.float32)
+    return high, mid, rest - mid
+
+
+def features(pan, is_row):
+    rows = []
     for axis in range(3):
-        r = three(row_pan[axis])
-        c = three(-2.0 * col_pan[axis])
+        value = pan[axis:axis + 1]
+        pieces = three(value if is_row else -2.0 * value)
         for i in range(3):
             for j in range(3):
                 if i + j < 4:
-                    left.append(r[i])
-                    right.append(c[j])
-    r_sq = three(jnp.sum(row_pan[:3] ** 2, 0))
-    c_sq = three(jnp.sum(col_pan[:3] ** 2, 0) + soft_sq)
-    one_r, one_c = jnp.ones_like(row_pan[0]), jnp.ones_like(col_pan[0])
-    for i in range(3):
-        left += [r_sq[i], one_r]
-        right += [one_c, c_sq[i]]
-    left += [jnp.zeros_like(one_r)] * 2
-    right += [jnp.zeros_like(one_c)] * 2
-    return jnp.stack(left).astype(jnp.bfloat16), jnp.stack(right).astype(jnp.bfloat16)
+                    rows.append(pieces[i if is_row else j])
+    square = pan[0:1] * pan[0:1] + pan[1:2] * pan[1:2] + pan[2:3] * pan[2:3]
+    one = jnp.ones_like(square)
+    for piece in three(square if is_row else square + soft_sq):
+        rows += [piece, one] if is_row else [one, piece]
+    return rows + [jnp.zeros_like(one)] * 2
 
 
 def flip(index, offset, count):
@@ -58,16 +53,17 @@
 
 def solve_kernel(
     depth, lines, cores, tile, unit, step_cols, kept,
-    b_ref, start_ref, scaled_ref, area_ref, diag_ref, left_ref, right_ref,
+    pan_ref, diag_ref, b_any, start_any,
     sol, res, hist_out,
+    pan_own, pan_held, feat, left_ref, right_ref, b_ref,
     vec, zdir, prev, direc, sdir, wide,
     sent, held, parts, chunk, chunk_in, sums, sums_in, sums_mid, sums_mid_in,
     slot_high, slot_low, kept_high, kept_low,
     vec_send, vec_recv, chunk_send, chunk_recv,
-    one_send, one_recv, two_send, two_recv, wide_send, wide_recv, start_sem,
+    one_send, one_recv, two_send, two_recv, wide_send, wide_recv, pan_send, pan_recv, load_sem,
 ):
     plane = lines * cores
-    cases, width = b_ref.shape
+    cases, width = vec.shape
     halves = width // unit
     per = width // step_cols
     gx = lax.axis_index("gx")
@@ -90,6 +86,30 @@
         pl.semaphore_signal(barrier, inc=1, device_id=in_line(k), device_id_type=MESH)
     pl.semaphore_wait(barrier, plane - 1 + depth - 1)
 
+    loads = (pltpu.make_async_copy(start_any, sol, load_sem.at[0]),
+             pltpu.make_async_copy(b_any.at[:, spot], b_ref, load_sem.at[1]))
+    for load in loads:
+        load.start()
+
+    def pan_copy(k):
+        return pltpu.make_async_remote_copy(
+            src_ref=pan_own, dst_ref=pan_held.at[k - 1],
+            send_sem=pan_send.at[k - 1], recv_sem=pan_recv.at[k - 1],
+            device_id=in_plane(k), device_id_type=MESH)
+
+    def fill(dst, index, pan, is_row):
+        for i, row in enumerate(features(pan, is_row)):
+            feat[i:i + 1, :] = row
+        dst[:, index * width:(index + 1) * width] = feat[...].astype(jnp.bfloat16)
+
+    def fill_from(k):
+        pan_copy(k).wait_recv()
+        fill(left_ref, k, pan_held[k - 1], True)
+
+    pan_own[...] = pan_ref[:, spot]
+    for k in range(1, plane):
+        pan_copy(k).start()
+
     def relayed(k):
         return k >= cores and k % cores > 0
 
@@ -135,9 +155,9 @@
 
     def build(high_ref, low_ref, k, half, col):
         right = right_ref[:, pl.ds(col, step_cols)]
-        base = flip(mine, k, plane) * width + half * unit
+        base = k * width + half * unit
         for sub in range(unit // tile):
-            left = left_ref[:, pl.ds(pl.multiple_of(base + sub * tile, tile), tile)]
+            left = left_ref[:, base + sub * tile:base + (sub + 1) * tile]
             value = lax.rsqrt(lax.dot_general(
                 left, right, (((0,), (0,)), ((), ())), preferred_element_type=jnp.float32))
             high = value.astype(jnp.bfloat16)
@@ -231,20 +251,24 @@
             sol[:, cols] = sol[:, cols] + alpha * ahead
             res[:, cols] = res[:, cols] - alpha * turned
 
-    fetch = pltpu.make_async_copy(start_ref, sol, start_sem)
-    fetch.start()
-    fetch.wait()
-    vec[...] = sol[:, spot]
     res[...] = jnp.zeros_like(res)
     direc[...] = jnp.zeros_like(direc)
     sdir[...] = jnp.zeros_like(sdir)
     zdir[...] = jnp.zeros_like(zdir)
     prev[...] = jnp.ones_like(prev)
     hist_out[...] = jnp.zeros_like(hist_out)
+    for g in range(depth):
+        fill(right_ref, g, pan_ref[:, g * width:(g + 1) * width], False)
+    fill(left_ref, 0, pan_own[...], True)
+    for k in range(1, NEAR):
+        fill_from(k)
+    for load in loads:
+        load.wait()
+    vec[...] = sol[:, spot]
 
     def step(turn, carry):
         par = lax.rem(turn, 2)
-        scaled = vec[...] * scaled_ref[...]
+        scaled = vec[...] * (pan_own[3:4, :] * (plane * depth * width) ** (-0.5))
         sent[par] = scaled
         for k in range(1, plane):
             if not relayed(k):
@@ -299,6 +323,12 @@
         for k in range(cores, plane, cores):
             split(k, held[par, k - 1])
         lax.fori_loop(split_at, count, near, 0)
+
+        @pl.when(turn == 0)
+        def _():
+            for k in range(NEAR, plane):
+                fill_from(k)
+
         for k in range(NEAR, plane):
             if k % cores:
                 vec_copy(par, k).wait_recv()
@@ -333,7 +363,7 @@
         for k in range(1, plane):
             vec_copy(par, k).wait_send()
         wide_finish(par)
-        image = diag_ref[...] * vec[...] + area_ref[...] * summed
+        image = diag_ref[:, spot] * vec[...] + pan_own[3:4, :] * summed
 
         @pl.when(turn == 0)
         def _():
@@ -364,12 +394,14 @@
     alpha, beta = factors(sums_finish(par), ITERS - 1)
     wide_finish(par)
     advance(par, alpha, beta)
-
-
-def solve(b_own, start, scaled, area, diag, left, right, depth, lines, cores):
-    cases, width = b_own.shape
+    for k in range(1, plane):
+        pan_copy(k).wait_send()
+
+
+def solve(panels, diagonal, right_side, start, depth, lines, cores):
+    cases, cols = right_side.shape
+    width = cols // depth
     plane = lines * cores
-    cols = right.shape[1]
     tile = min(256, width)
     unit = min(UNIT, width)
     step_cols = min(STEP, width)
@@ -388,9 +420,12 @@
             jax.ShapeDtypeStruct((cases, cols), f32),
             jax.ShapeDtypeStruct((cases, 128), f32),
         ),
-        in_specs=[whole, pl.BlockSpec(memory_space=pl.ANY)] + [whole] * 5,
+        in_specs=[whole] * 2 + [pl.BlockSpec(memory_space=pl.ANY)] * 2,
         out_specs=(whole,) * 3,
         scratch_shapes=[
+            pltpu.VMEM((4, width), f32), pltpu.VMEM((plane - 1, 4, width), f32),
+            pltpu.VMEM((32, width), f32), pltpu.VMEM((32, plane * width), jnp.bfloat16),
+            pltpu.VMEM((32, cols), jnp.bfloat16), state,
             state, state, pltpu.VMEM((cases, 128), f32),
             pltpu.VMEM((depth, cases, width), f32), pltpu.VMEM((depth, cases, width), f32),
             pltpu.VMEM((2, depth, cases, width), f32),
@@ -408,35 +443,18 @@
             dma((2, depth)), dma((2, depth)),
             dma((2, depth - 1)), dma((2, depth - 1)),
             dma((2, plane - 1)), dma((2, plane - 1)),
-            dma((2, depth - 1)), dma((2, depth - 1)), dma(()),
+            dma((2, depth - 1)), dma((2, depth - 1)),
+            dma((plane - 1,)), dma((plane - 1,)), dma((2,)),
         ],
         compiler_params=pltpu.CompilerParams(
             collective_id=0, has_side_effects=True, vmem_limit_bytes=67043328),
-    )(b_own, start, scaled, area, diag, left, right)
+    )(panels, diagonal, right_side, start)
 
 
 def on_device(panels, diagonal, right_side, start_guess):
-    col_count = panels.shape[1]
-    depth = lax.axis_size("gx")
-    lines = lax.axis_size("gy")
-    cores = lax.axis_size("gz")
-    total = col_count * lines * cores
-    width = col_count // depth
-    mine = lax.axis_index("gx") * width
-
-    def own(value):
-        return lax.dynamic_slice_in_dim(value, mine, width, value.ndim - 1)
-
-    pan_own = own(panels)
-    diag_own = own(diagonal)[None, :]
-    area_own = pan_own[3][None, :]
-    scaled_area = area_own * total ** (-0.5)
-    row_pan = lax.all_gather(pan_own, PLANE, axis=0)
-    row_pan = jnp.swapaxes(row_pan, 0, 1).reshape(4, -1)
-    left, right = features(row_pan, panels)
     solution, residual, records = solve(
-        own(right_side), start_guess, scaled_area, area_own, diag_own,
-        left, right, depth, lines, cores)
+        panels, diagonal[None, :], right_side, start_guess,
+        lax.axis_size("gx"), lax.axis_size("gy"), lax.axis_size("gz"))
     return solution, residual, records[:, :ITERS].T
 
 

time: 242 us -> 219 us (0.905)
  local copies, waits for them, and re-layouts: 15.2 us -> 4.1 us
  blocking collectives: 10.7 us -> 0 us
    all_gather x1 -> x0, blocking collectives: 10.7 us -> none  [on_device(): row_pan = lax.all_gather(pan_own, PLANE, axis=0)]
    another operation x6 -> x0, local copies, waits for them, and re-layouts: 7.41 us -> none  [the longest x2 4.11 us: features(): jnp.stack(left).astype(jnp.bfloat16)]
    dynamic_slice x2 -> x0, local copies, waits for them, and re-layouts: 2.88 us -> none  [own(): return lax.dynamic_slice_in_dim(value, mine, width, value.ndim - 1)]
where the time goes in v3:
time: 219 us
  Pallas kernels  214 us (98%)
  local copies, waits for them, and re-layouts  4.1 us (2%)
    pallas_call x1, Pallas kernels, solve(): pl.pallas_call(functools.partial(solve_kernel, depth, lines, cores, tile,...  214 us

profile of v3, /device:TPU:0, one launch (start us, length us, event | category | flops | bytes accessed | tf_op | source)
XLA Modules:
  0.0 219.1 jit_solution(9283180108421628115)
XLA Ops:
  0.6 214.4 %shard_map.67 = (f32[32,4096]{1,0:T(8,128)}, f32[32,4096]{1,0:T(8,128)}, f32[32,128]{1,0:T(8,128)}) custom-call(f32[4,4096]{1,0:T(4,128)} %pan_ref.1, f32[1,4096]{1,0:T(1,128)} %bitcast.3, f32[32,4096]{1,0:T(8,128)} %b_any.1, f32[32,4096]{1,0:T(8,128)} %start_any.1), custom_call_target="tpu_custom_call" | custom-call | tf_op jit(solution)/shard_map/pallas_call | solution.py:416
  215.0 0.7 slice_bitcast_fusion
  215.7 0.7 copy.7
  216.4 0.0 copy-start
  216.4 1.9 copy.10
  218.3 0.0 copy-done
  218.3 0.8 copy.11
Async XLA Ops:
  216.4 1.9 copy-start
